TPU v7x, 128 devices: a whole 4x4x4 slice. The times are simulated.
128 devices in a mesh: stage: 4 (over x), expert: 32 (over z, y, core).
Axes of the slice: x: 4, y: 4, z: 4, core: 2. Of those that a mesh axis runs over, the one named last changes fastest.
Arguments:
- w_gate: bfloat16 [4, 32, 1024, 512], P('stage', 'expert')
- w_up: bfloat16 [4, 32, 1024, 512], P('stage', 'expert')
- w_down: bfloat16 [4, 32, 512, 1024], P('stage', 'expert')
- dense: bfloat16 [4, 1024, 1024], P('stage')
- hot_ids: int32 [2], replicated
- spare_map: int32 [128], P(('stage', 'expert'))
Outputs:
- output 1: bfloat16 [4, 128, 1024, 256], P(None, ('stage', 'expert'))
- output 2: bfloat16 [4, 128, 128, 1024], P(None, ('stage', 'expert'))
- output 3: bfloat16 [4, 1024, 1024], replicated
- output 4: bfloat16 [4, 128, 1024, 256], P(None, ('stage', 'expert'))
- output 5: bfloat16 [4, 128, 128, 1024], P(None, ('stage', 'expert'))
All inputs are finite; a program needn't handle non-finite values.
Results may differ from a plain program's by a relative error of at most 0.001.
Values are sent between devices in bfloat16 or wider.
A program may use at most 1 GiB of HBM per device.

v0:
```python
import jax
import jax.numpy as jnp
from jax import lax
from jax.sharding import PartitionSpec as P


def solution(mesh):
    stage_count = mesh.shape['stage']
    group_count = mesh.shape['expert']
    device_count = stage_count * group_count
    flat_axes = ('stage', 'expert')
    pair_list = [(pos * group_count + col, col * stage_count + pos) for pos in range(stage_count) for col in range(group_count)]

    def local_move(w_gate, w_up, w_down, dense, hot_ids, spare_map):
        layer_local, expert_local, d_model, ff_width = w_gate.shape
        expert_total = expert_local * group_count
        pieces = max(1, device_count // expert_total)
        piece_width = ff_width // pieces
        unit_local = expert_local * pieces
        gate_parts = w_gate.reshape(layer_local, expert_local, d_model, pieces, piece_width)
        up_parts = w_up.reshape(layer_local, expert_local, d_model, pieces, piece_width)
        gate_up = jnp.concatenate([gate_parts, up_parts], axis=-1)
        gate_up = jnp.transpose(gate_up, (0, 1, 3, 2, 4)).reshape(layer_local, unit_local, d_model, 2 * piece_width)
        down_units = w_down.reshape(layer_local, unit_local, piece_width, d_model)

        local_ids = lax.axis_index('expert') * unit_local + jnp.arange(unit_local)
        owned_mask = (hot_ids[:, None] == local_ids[None, :]).astype(jnp.bfloat16)
        hot_gate_up = jnp.einsum('hu,ludf->lhdf', owned_mask, gate_up, preferred_element_type=jnp.float32).astype(jnp.bfloat16)
        hot_down = jnp.einsum('hu,lufd->lhfd', owned_mask, down_units, preferred_element_type=jnp.float32).astype(jnp.bfloat16)
        hot_gate_up = lax.psum(hot_gate_up, 'expert')
        hot_down = lax.psum(hot_down, 'expert')
        hot_gate_up = lax.all_gather(hot_gate_up, 'stage', axis=0, tiled=True)
        hot_down = lax.all_gather(hot_down, 'stage', axis=0, tiled=True)
        slot_pick = (spare_map[:, None] == jnp.arange(hot_ids.shape[0])[None, :]).astype(jnp.bfloat16)
        spare_gate_up = jnp.einsum('nh,lhdf->lndf', slot_pick, hot_gate_up, preferred_element_type=jnp.float32).astype(jnp.bfloat16)
        spare_down = jnp.einsum('nh,lhfd->lnfd', slot_pick, hot_down, preferred_element_type=jnp.float32).astype(jnp.bfloat16)

        gate_up = lax.all_to_all(gate_up, 'stage', 1, 0, tiled=True)
        down_units = lax.all_to_all(down_units, 'stage', 1, 0, tiled=True)
        gate_up = lax.ppermute(gate_up, flat_axes, pair_list)
        down_units = lax.ppermute(down_units, flat_axes, pair_list)
        dense_all = lax.all_gather(dense, 'stage', axis=0, tiled=True)
        return gate_up, down_units, dense_all, spare_gate_up, spare_down

    expert_spec = P('stage', 'expert', None, None)
    unit_spec = P(None, flat_axes, None, None)
    return jax.shard_map(
        local_move,
        mesh=mesh,
        in_specs=(expert_spec, expert_spec, expert_spec, P('stage', None, None), P(None), P(flat_axes)),
        out_specs=(unit_spec, unit_spec, P(None, None, None), unit_spec, unit_spec),
        check_vma=False,
    )
```

profile of v0, /device:TPU:127, one launch (start us, length us, event | category | flops | bytes accessed | tf_op | source)
XLA Modules:
  0.0 459.8 jit_solution(260692153347939827)
XLA Ops:
  7.2 0.0 all-reduce.3.cloned.1.call-start
  7.2 1.3 reshape.60
  8.6 0.4 constant_dynamic-update-slice_fusion.1
  9.0 0.0 copy-start.3
  9.0 1.3 reshape.61
  10.3 0.0 copy-start
  10.3 0.7 constant_dynamic-update-slice_fusion
  11.1 0.0 copy-done.3
  11.1 0.5 copy-done
  11.5 1.8 fusion.13
  13.3 2.3 fusion.10
  15.6 0.0 all-reduce.3.cloned.1.call-update
  15.6 0.0 all-gather.8.cloned.1.call-start
  15.6 106.4 %all-reduce.3.cloned.1.call-done = (bf16[1,2,1024,256]{3,1,2,0:T(2,128)(2,1)}, bf16[1,2,128,1024]{3,1,2,0:T(2,128)(2,1)}) async-done(((bf16[1,2,1024,256]{3,1,2,0:T(2,128)(2,1)}, bf16[1,2,128,1024]{3,1,2,0:T(2,128)(2,1)}), (bf16[1,2,1024,256]{3,1,2,0:T(2,128)(2,1)}, bf16[1,2,128,1024]{3,1,2,0:T(2,128)(2,1)})) %all-reduce.3.cloned.1.call-update) | async-done | bytes 1572880 | tf_op jit(solution)/shard_map/psum | solution.py:30
  122.1 0.0 copy-start.2
  122.1 2.0 copy.16
  124.1 0.0 all-gather.8.cloned.1.call-update
  124.1 0.0 all-gather.6.cloned.1.call-start
  124.2 0.0 copy-done.2
  124.2 1.1 copy.14
  125.3 0.0 all-gather.6.cloned.1.call-update
  125.3 0.0 all-gather.4.cloned.1.call-start
  125.4 0.5 all-gather.4.cloned.1.call-update
  125.9 0.3 copy.13
  126.2 0.0 copy-start.1
  126.2 45.4 %all_to_all.24 = bf16[1,4,1024,256]{3,2,0,1:T(8,128)(2,1)S(1)} all-to-all(bf16[1,4,1024,256]{3,2,0,1:T(8,128)(2,1)S(1)} %copy.13), channel_id=1, replica_groups=mesh['stage'=4,'expert'=32] {'stage'}, dimensions={1} | all-to-all | bytes 4194304 | tf_op jit(solution)/shard_map/all_to_all | solution.py:38
  171.6 0.8 collective-permute-start
  172.4 0.0 copy-done.1
  172.4 138.7 %all_to_all.25 = bf16[1,4,128,1024]{3,2,0,1:T(8,128)(2,1)S(1)} all-to-all(bf16[1,4,128,1024]{3,2,0,1:T(8,128)(2,1)S(1)} %bitcast.69), channel_id=1, replica_groups=mesh['stage'=4,'expert'=32] {'stage'}, dimensions={1} | all-to-all | bytes 2097152 | tf_op jit(solution)/shard_map/all_to_all | solution.py:39
  311.0 0.9 collective-permute-start.1
  312.6 0.0 collective-permute-done.1
  312.6 0.0 collective-permute-done
  312.6 0.0 all-gather.8.cloned.1.call-done
  312.7 3.9 fusion.5
  316.6 1.3 copy.38
  317.9 0.0 all-gather.6.cloned.1.call-done
  317.9 21.1 %fusion = bf16[1,4,1024,256]{3,0,2,1:T(2,128)(2,1)S(1)} fusion(bf16[4,2,1024,256]{3,2,1,0:T(8,128)(2,1)} %all-gather.6.cloned.1.call-done, s32[]{:T(128)} %bitcast.61), kind=kOutput, calls=%fused_computation.1 | convolution fusion | flops 4194306 | bytes 6291460 | tf_op jit(solution)/shard_map/nh,lhdf->lndf/dot_general | solution.py:35
  339.1 1.8 copy.37
  340.8 102.4 %all-gather.4.cloned.1.call-done = bf16[4,1024,1024]{2,1,0:T(8,128)(2,1)} async-done(((bf16[1,1024,1024]{2,1,0:T(8,128)(2,1)}), bf16[4,1024,1024]{2,1,0:T(8,128)(2,1)}) %all-gather.4.cloned.1.call-update) | async-done | bytes 8388624 | tf_op jit(solution)/shard_map/all_gather | solution.py:42
  443.2 1.3 copy.46
  444.6 1.0 copy.47
  445.5 7.8 %copy.48 = bf16[4,1024,1024]{2,1,0:T(8,128)(2,1)} copy(bf16[4,1024,1024]{2,1,0:T(8,128)(2,1)} %all-gather.4.cloned.1.call-done) | data formatting | bytes 16777216
  (1 shorter events, 0.0 us)
Async XLA Ops:
  7.2 114.9 %all-reduce.3.cloned.1.call-start = ((), (), s32[]{:S(2)}) async-start(), calls=%async_computation.5 | async-start | bytes 3145728 | tf_op jit(solution)/shard_map/psum | solution.py:30
  9.0 2.1 copy-start.3
  10.3 1.2 copy-start
  15.6 297.0 %all-gather.8.cloned.1.call-start = ((), (), s32[]{:S(2)}) async-start(), calls=%async_computation.4 | async-start | bytes 2621440 | tf_op jit(solution)/shard_map/all_gather | solution.py:33
  122.1 2.1 copy-start.2
  124.1 193.8 %all-gather.6.cloned.1.call-start = ((), (), s32[]{:S(2)}) async-start(), calls=%async_computation.3 | async-start | bytes 5242880 | tf_op jit(solution)/shard_map/all_gather | solution.py:32
  125.3 317.9 %all-gather.4.cloned.1.call-start = ((), (), s32[]{:S(2)}) async-start(), calls=%async_computation.2 | async-start | bytes 10485760 | tf_op jit(solution)/shard_map/all_gather | solution.py:42
  126.2 46.2 %copy-start.1 = (bf16[1,1,512,1024]{3,2,1,0:T(8,128)(2,1)S(1)}, bf16[1,1,512,1024]{3,2,1,0:T(8,128)(2,1)}, u32[]{:S(2)}) copy-start(bf16[1,1,512,1024]{3,2,1,0:T(8,128)(2,1)} %param.8) | copy-start | bytes 3145732
  171.6 141.0 %collective-permute-start = (bf16[4,1,1024,256]{3,2,0,1:T(8,128)(2,1)S(1)}, bf16[4,1,1024,256]{3,2,0,1:T(8,128)(2,1)S(1)}, u32[]{:S(2)}, u32[]{:S(2)}) collective-permute-start(bf16[4,1,1024,256]{3,2,0,1:T(8,128)(2,1)S(1)} %bitcast.66), channel_id=1, source_target_pairs={{0,0},{1,4},{2,8},{3,12},{4,16},{5,20},{6,24},{7,28},{8,32},{9,36}... | collective-permute-start | bytes 6291464 | tf_op jit(solution)/shard_map/ppermute | solution.py:40
  311.0 1.6 collective-permute-start.1
Sparse Core Ops, SparseCore 0:
  15.7 106.2 all-reduce.2
  124.3 46.2 all-gather.7
  172.9 122.9 all-gather.5
  297.3 145.8 all-gather.3
where the time goes:
time: 460 us
  waiting for transfers between devices  209 us (45%)
  blocking collectives  184 us (40%)
  matrix products  29.1 us (6%)
  local copies, waits for them, and re-layouts  20.8 us (5%)
  between operations  14.6 us (3%)
    all_to_all x1, blocking collectives, local_move(): down_units = lax.all_to_all(down_units, 'stage', 1, 0, tiled=True)  139 us
    psum x1, waiting for transfers between devices, local_move(): hot_gate_up = lax.psum(hot_gate_up, 'expert')  106 us
    all_gather x1, waiting for transfers between devices, local_move(): dense_all = lax.all_gather(dense, 'stage', axis=0, tiled=True)  102 us
    all_to_all x1, blocking collectives, local_move(): gate_up = lax.all_to_all(gate_up, 'stage', 1, 0, tiled=True)  45.4 us
    dot_general x1, matrix products, local_move(): jnp.einsum('nh,lhdf->lndf', slot_pick, hot_gate_up, preferred_element_typ...  21.1 us
    unnamed x12, local copies, waits for them, and re-layouts  10.9 us
  transfers between devices with their start and end apart: 6, of which 2 were waited for; matrix products, arithmetic and copies ran while one was open for 6% of the time, Pallas kernels for 0%

commit v1 on v0

v1 whole, which is shorter than its diff:
```python
import functools

import jax
import jax.numpy as jnp
from jax import lax
from jax.experimental import pallas as pl
from jax.experimental.pallas import tpu as pltpu
from jax.sharding import PartitionSpec as P

MESH = pl.DeviceIdType.MESH
BF16 = jnp.bfloat16
RING = 4
UNIT_CHUNKS = 6
DENSE_CHUNKS = 8


def _exchange(gate, up, down, dense, hot, b13, b2, h13, h2, dn,
              w13, w2, p13, p2, q13, q2, c13, c2, rz13, rz2, s13, s2, ry13, ry2, ss, rs, ls):
    x = lax.axis_index('stage')
    e = lax.axis_index('expert')
    z, y, c = e // 8, (e % 8) // 2, e % 2

    def dev(xx, yy, zz, cc):
        return (lax.rem(xx + RING, RING), lax.rem(zz + RING, RING) * 8 + lax.rem(yy + RING, RING) * 2 + cc)

    def ring(v):
        return lax.rem(v + RING, RING)

    partner = dev(x, y, z, 1 - c)
    counter = [0]
    pending = []

    def slots(n):
        base = counter[0]
        counter[0] += n
        return base

    def remote(src, dst, device, slot=None, recv=None):
        slot = slots(1) if slot is None else slot
        recv = slot if recv is None else recv
        return pltpu.make_async_remote_copy(src_ref=src, dst_ref=dst, send_sem=ss.at[slot], recv_sem=rs.at[recv],
                                            device_id=device, device_id_type=MESH)

    def go(*copies):
        for copy in copies:
            copy.start()
            pending.append(copy)

    stays = (z == y) & (c == y // 2)

    def land(zs):
        return jnp.where(zs == x, x, RING + zs)

    loads = []
    for p in range(4):
        cols = pl.ds(p * 128, 128)
        loads.append(pltpu.make_async_copy(gate.at[:, :, :, cols], w13.at[p, :, :, :, 0:128], ls.at[p]))
        loads.append(pltpu.make_async_copy(up.at[:, :, :, cols], w13.at[p, :, :, :, 128:256], ls.at[4 + p]))
    loads.append(pltpu.make_async_copy(down, w2, ls.at[8]))
    load_dense = pltpu.make_async_copy(dense, dn.at[x], ls.at[9])
    own_piece = 2 * (y % 2) + c
    own_cols = pl.ds(pl.multiple_of(own_piece * 128, 128), 128)
    keep = [
        pltpu.make_async_copy(gate.at[:, :, :, own_cols], b13.at[land(z), :, :, :, 0:128], ls.at[10]),
        pltpu.make_async_copy(up.at[:, :, :, own_cols], b13.at[land(z), :, :, :, 128:256], ls.at[11]),
        pltpu.make_async_copy(down.at[own_piece], b2.at[land(z)], ls.at[12]),
    ]
    for copy in loads:
        copy.start()
    load_dense.start()

    @pl.when(stays)
    def _():
        for copy in keep:
            copy.start()

    bar = pltpu.get_barrier_semaphore()

    def greet(device):
        pl.semaphore_signal(bar, inc=1, device_id=device, device_id_type=MESH)

    for zs in range(RING):
        @pl.when(jnp.logical_not(stays & (z == zs)))
        def _():
            greet(dev(x, z, zs, y // 2))
    for d in (1, 2, 3):
        greet(dev(x + d, y, z, c))
        greet(dev(x, y + d, z, c))
        greet(dev(x, y, z + d, c))
    greet(partner)

    for copy in loads:
        copy.wait()
    hot_c = hot[c]
    hot_n = hot[1 - c]
    p13[...] = w13[hot_n % 4]
    p2[...] = w2[hot_n % 4]
    pl.semaphore_wait(bar, jnp.where(stays, 13, 14))

    yz_send = slots(4 * UNIT_CHUNKS)
    yz_recv = slots(4 * UNIT_CHUNKS)

    def unit_part(big, small, index, q):
        if q < 4:
            return big.at[index, q]
        return small.at[index, pl.ds(2 * (q - 4), 2)]

    def yz(p, q):
        return remote(unit_part(w13, w2, p, q), unit_part(b13, b2, land(z), q),
                      dev(x, 2 * c + p // 2, y, p % 2), yz_send + p * UNIT_CHUNKS + q, yz_recv + z * UNIT_CHUNKS + q)

    def yz_self(p):
        return stays & (own_piece == p)

    def yz_go(q):
        for p in range(4):
            @pl.when(jnp.logical_not(yz_self(p)))
            def _():
                yz(p, q).start()

    def yz_drain():
        for q in range(UNIT_CHUNKS):
            for p in range(4):
                @pl.when(jnp.logical_not(yz_self(p)))
                def _():
                    yz(p, q).wait_send()

    def yz_arrive(zs, q):
        part = unit_part(b13, b2, land(zs), q)

        @pl.when(jnp.logical_not(stays & (zs == z)))
        def _():
            remote(part, part, partner, yz_send, yz_recv + zs * UNIT_CHUNKS + q).wait_recv()

        if q == 0:
            @pl.when(stays & (zs == z))
            def _():
                for copy in keep:
                    copy.wait()

    def x_make(d, q):
        to = ring(x + d)
        return remote(unit_part(b13, b2, RING + to, q), unit_part(b13, b2, x, q), dev(x + d, y, z, c))

    x_copies = {(d, q): x_make(d, q) for d in (1, 2, 3) for q in range(UNIT_CHUNKS)}

    def x_go(q):
        for d in (1, 3, 2):
            yz_arrive(ring(x + d), q)
            go(x_copies[d, q])

    def dn_part(layer, j, core=None):
        return dn.at[layer, c if core is None else core, j]

    half = DENSE_CHUNKS // 2
    d_right = [remote(dn_part(x, j), dn_part(x, j), dev(x + 1, y, z, c)) for j in range(DENSE_CHUNKS)]
    d_left = [remote(dn_part(x, j), dn_part(x, j), dev(x - 1, y, z, c)) for j in range(DENSE_CHUNKS)]
    d_far = [remote(dn_part(ring(x - 1), j), dn_part(ring(x - 1), j), dev(x + 1, y, z, c)) if j < half else
             remote(dn_part(ring(x + 1), j), dn_part(ring(x + 1), j), dev(x - 1, y, z, c)) for j in range(DENSE_CHUNKS)]
    d_pass = {(d, j): remote(dn_part(ring(x + d), j), dn_part(ring(x + d), j), partner)
              for d in (1, 2, 3) for j in range(DENSE_CHUNKS)}

    def dense_start():
        load_dense.wait()
        for i in range(DENSE_CHUNKS):
            go(d_right[i], d_left[(i + half) % DENSE_CHUNKS])

    def dense_near(i):
        j = (i + half) % DENSE_CHUNKS
        d_right[i].wait_recv()
        if i < half:
            go(d_far[i])
        go(d_pass[3, i])
        d_left[j].wait_recv()
        if j >= half:
            go(d_far[j])
        go(d_pass[1, j])

    def dense_far():
        for j in range(DENSE_CHUNKS):
            d_far[j].wait_recv()
            go(d_pass[2, j])

    def dense_end():
        for copy in d_pass.values():
            copy.wait_recv()

    pq = [remote(p13, q13, partner), remote(p2, q2, partner)]
    rsz = {d: [remote(c13.at[:, ring(z + d)], rz13.at[z], dev(x, y, z + d, c)),
               remote(c2.at[:, ring(z + d)], rz2.at[z], dev(x, y, z + d, c))] for d in (1, 2, 3)}
    rsy = {d: [remote(s13.at[ring(y + d)], ry13.at[y], dev(x, y + d, z, c)),
               remote(s2.at[ring(y + d)], ry2.at[y], dev(x, y + d, z, c))] for d in (1, 2, 3)}
    agx = {d: [remote(h.at[c, x, y, z], h.at[c, x, y, z], dev(x + d, y, z, c)) for h in (h13, h2)] for d in (1, 2, 3)}
    ag1 = {d: [remote(h.at[c, 0:2, y, z], h.at[c, 0:2, y, z], dev(x, y, z + d, c)) for h in (h13, h2)]
           + [remote(h.at[c, 2:4, y, z], h.at[c, 2:4, y, z], dev(x, y + d, z, c)) for h in (h13, h2)] for d in (1, 2, 3)}

    def block(h, layer, d):
        if layer < 2:
            return h.at[c, layer, ring(y + d)]
        return h.at[c, layer, :, ring(z + d)]

    def along(layer, d):
        return dev(x, y + d, z, c) if layer < 2 else dev(x, y, z + d, c)

    ag2 = {(d, l): [remote(block(h, l, 0), block(h, l, 0), along(l, d)) for h in (h13, h2)] for d in (1, -1) for l in range(4)}
    ag3 = {l: [remote(block(h, l, -1 if l % 2 == 0 else 1), block(h, l, -1 if l % 2 == 0 else 1),
                      along(l, 1 if l % 2 == 0 else -1)) for h in (h13, h2)] for l in range(4)}
    h_pass = {(d, l): [remote(block(h, l, d), block(h, l, d), partner) for h in (h13, h2)]
              for d in (0, 1, 2, 3) for l in range(4)}

    def recv(copies):
        for copy in copies:
            copy.wait_recv()

    def hot_swap():
        go(*pq)

    def hot_rsz():
        recv(pq)
        own = (hot_c // 4) % 2 == c
        c13[...] = jnp.where(own, w13[hot_c % 4], q13[...])
        c2[...] = jnp.where(own, w2[hot_c % 4], q2[...])
        rz13[z] = c13[:, z]
        rz2[z] = c2[:, z]
        for d in (1, 3, 2):
            go(*rsz[d])

    def hot_rsy():
        for d in (1, 3, 2):
            recv(rsz[d])
        zh = hot_c // 32
        s13[...] = rz13[zh]
        s2[...] = rz2[zh]
        ry13[y] = s13[y]
        ry2[y] = s2[y]
        for d in (1, 3, 2):
            go(*rsy[d])

    def hot_agx():
        for d in (1, 3, 2):
            recv(rsy[d])
        yh = (hot_c // 8) % 4
        h13[c, x, y, z] = ry13[yh]
        h2[c, x, y, z] = ry2[yh]
        for d in (1, 3, 2):
            go(*agx[d])

    def hot_ag1():
        for d in (1, 3, 2):
            recv(agx[d])
        for d in (1, 3, 2):
            go(*ag1[d])

    def hot_ag2():
        for d in (1, 3, 2):
            recv(ag1[d])
        for l in (0, 2):
            go(*ag2[1, l])
            go(*ag2[-1, l + 1])
        for l in (1, 3):
            go(*ag2[1, l])
            go(*ag2[-1, l - 1])
        for l in range(4):
            go(*h_pass[0, l])

    def hot_ag3():
        for l in (0, 2):
            recv(ag2[1, l])
            go(*ag3[l])
            recv(ag2[-1, l + 1])
            go(*ag3[l + 1])
        for l in (0, 2):
            go(*h_pass[3, l])
            go(*h_pass[1, l + 1])
        for l in (1, 3):
            recv(ag2[1, l])
            go(*h_pass[3, l])
            recv(ag2[-1, l - 1])
            go(*h_pass[1, l - 1])

    def hot_end():
        for l in range(4):
            recv(ag3[l])
            go(*h_pass[2, l])
        for copies in h_pass.values():
            recv(copies)

    hot_swap()
    yz_go(0)
    dense_start()
    hot_rsz()
    yz_go(1)
    yz_go(2)
    hot_rsy()
    yz_go(3)
    dense_near(0)
    x_go(0)
    hot_agx()
    yz_go(4)
    yz_go(5)
    dense_near(1)
    dense_near(2)
    x_go(1)
    hot_ag1()
    dense_near(3)
    x_go(2)
    for i in range(4, 8):
        dense_near(i)
    hot_ag2()
    x_go(3)
    hot_ag3()
    x_go(4)
    x_go(5)
    dense_far()
    hot_end()
    dense_end()
    for q in range(UNIT_CHUNKS):
        yz_arrive(x, q)
    for copy in x_copies.values():
        copy.wait_recv()
    yz_drain()
    for copy in pending:
        copy.wait_send()


def _write(spare, b13, b2, h13, h2, dn, o13, o2, odn, osp13, osp2, zero13, zero2, sem):
    copies = [
        pltpu.make_async_copy(dn, odn, sem.at[0]),
        pltpu.make_async_copy(b13.at[0:4], o13, sem.at[1]),
        pltpu.make_async_copy(b2.at[0:4], o2, sem.at[2]),
    ]
    for copy in copies:
        copy.start()
    slot = spare[0]

    @pl.when(slot >= 0)
    def _():
        fill = [pltpu.make_async_copy(h13.at[slot], osp13, sem.at[3]), pltpu.make_async_copy(h2.at[slot], osp2, sem.at[4])]
        for copy in fill:
            copy.start()
        for copy in fill:
            copy.wait()

    @pl.when(slot < 0)
    def _():
        zero13[...] = jnp.zeros_like(zero13)
        zero2[...] = jnp.zeros_like(zero2)
        fill = [pltpu.make_async_copy(zero13, osp13.at[l, m], sem.at[5 + 4 * l + m]) for l in range(4) for m in range(4)]
        fill += [pltpu.make_async_copy(zero2, osp2.at[l], sem.at[21 + l]) for l in range(4)]
        for copy in fill:
            copy.start()
        for copy in fill:
            copy.wait()

    for copy in copies:
        copy.wait()


def solution(mesh):
    flat_axes = ('stage', 'expert')

    def local_move(w_gate, w_up, w_down, dense, hot_ids, spare_map):
        gate = w_gate.reshape(4, 4, 64, 512)
        up = w_up.reshape(4, 4, 64, 512)
        down = w_down.reshape(4, 4, 4, 8, 1024)
        dense_in = dense.reshape(2, DENSE_CHUNKS, 64, 1024)
        hbm = pl.BlockSpec(memory_space=pltpu.HBM)
        vmem = pl.BlockSpec(memory_space=pltpu.VMEM)
        smem = pl.BlockSpec(memory_space=pltpu.SMEM)
        count = 400
        moved = pl.pallas_call(
            _exchange,
            name='exchange',
            out_shape=(
                pltpu.VMEM((8, 4, 4, 64, 256), BF16),
                pltpu.VMEM((8, 4, 4, 8, 1024), BF16),
                pltpu.VMEM((2, 4, 4, 4, 64, 256), BF16),
                pltpu.VMEM((2, 4, 4, 4, 8, 1024), BF16),
                pltpu.VMEM((4, 2, DENSE_CHUNKS, 64, 1024), BF16),
            ),
            in_specs=[hbm] * 4 + [smem],
            out_specs=[vmem] * 5,
            scratch_shapes=[
                pltpu.VMEM((4, 4, 4, 64, 256), BF16), pltpu.VMEM((4, 4, 4, 8, 1024), BF16),
                pltpu.VMEM((4, 4, 64, 256), BF16), pltpu.VMEM((4, 4, 8, 1024), BF16),
                pltpu.VMEM((4, 4, 64, 256), BF16), pltpu.VMEM((4, 4, 8, 1024), BF16),
                pltpu.VMEM((4, 4, 64, 256), BF16), pltpu.VMEM((4, 4, 8, 1024), BF16),
                pltpu.VMEM((4, 4, 64, 256), BF16), pltpu.VMEM((4, 4, 8, 1024), BF16),
                pltpu.VMEM((4, 64, 256), BF16), pltpu.VMEM((4, 8, 1024), BF16),
                pltpu.VMEM((4, 64, 256), BF16), pltpu.VMEM((4, 8, 1024), BF16),
                pltpu.SemaphoreType.DMA((count,)), pltpu.SemaphoreType.DMA((count,)), pltpu.SemaphoreType.DMA((13,)),
            ],
            compiler_params=pltpu.CompilerParams(collective_id=0, has_side_effects=True, vmem_limit_bytes=16 * 2**20),
        )(*[pltpu.with_memory_space_constraint(part, pltpu.HBM) for part in (gate, up, down, dense_in)], hot_ids)
        moved = [pltpu.with_memory_space_constraint(part, pltpu.VMEM) for part in moved]
        o13, o2, odn, osp13, osp2 = pl.pallas_call(
            _write,
            name='write',
            out_shape=(
                jax.ShapeDtypeStruct((4, 4, 4, 64, 256), BF16),
                jax.ShapeDtypeStruct((4, 4, 4, 8, 1024), BF16),
                jax.ShapeDtypeStruct((4, 2, DENSE_CHUNKS, 64, 1024), BF16),
                jax.ShapeDtypeStruct((4, 4, 4, 64, 256), BF16),
                jax.ShapeDtypeStruct((4, 4, 4, 8, 1024), BF16),
            ),
            in_specs=[smem] + [vmem] * 5,
            out_specs=[hbm] * 5,
            scratch_shapes=[pltpu.VMEM((4, 64, 256), BF16), pltpu.VMEM((4, 4, 8, 1024), BF16), pltpu.SemaphoreType.DMA((25,))],
            compiler_params=pltpu.CompilerParams(vmem_limit_bytes=4 * 2**20),
        )(spare_map, *moved)
        return (o13.reshape(4, 1, 1024, 256), o2.reshape(4, 1, 128, 1024), odn.reshape(4, 1024, 1024),
                osp13.reshape(4, 1, 1024, 256), osp2.reshape(4, 1, 128, 1024))

    expert_spec = P('stage', 'expert', None, None)
    unit_spec = P(None, flat_axes, None, None)
    return jax.shard_map(
        local_move,
        mesh=mesh,
        in_specs=(expert_spec, expert_spec, expert_spec, P('stage', None, None), P(None), P(flat_axes)),
        out_specs=(unit_spec, unit_spec, P(None, None, None), unit_spec, unit_spec),
        check_vma=False,
    )
```

time: 460 us -> 102 us (0.22)
  the two profiles are of different devices: /device:TPU:127 before, /device:TPU:8 now
where the time goes in v1:
time: 102 us
  Pallas kernels  99.9 us (98%)
  between operations  1.3 us (1%)
    pallas_call x1, Pallas kernels, local_move(): pl.pallas_call(_exchange, name='exchange', out_shape=(pltpu.VMEM((8, 4, 4...  94.4 us
    pallas_call x1, Pallas kernels, local_move(): pl.pallas_call(_write, name='write', out_shape=(jax.ShapeDtypeStruct((4,...  5.5 us

profile of v1, /device:TPU:8, one launch (start us, length us, event | category | flops | bytes accessed | tf_op | source)
XLA Modules:
  0.0 101.8 jit_solution(3705594931890700993)
XLA Ops:
  1.3 0.0 copy-start
  1.3 0.6 copy-done
  1.9 94.4 %exchange.1 = (bf16[8,4,4,64,256]{4,3,2,1,0:T(8,128)(2,1)S(1)}, bf16[8,4,4,8,1024]{4,3,2,1,0:T(8,128)(2,1)S(1)}, bf16[2,4,4,4,64,256]{5,4,3,2,1,0:T(8,128)(2,1)S...) custom-call(bf16[4,4,64,512]{3,2,1,0:T(8,128)(2,1)} %bitcast.18, ...), custom_call_target="tpu_custom_call" | custom-call | tf_op jit(solution)/shard_map/exchange/pallas_call | solution.py:371
  96.3 5.5 %write.1 = (bf16[4,4,4,64,256]{4,3,2,1,0:T(8,128)(2,1)}, bf16[4,4,4,8,1024]{4,3,2,1,0:T(8,128)(2,1)}, bf16[4,2,8,64,1024]{4,3,2,1,0:T(8,128)(2,1)}, bf16[4,4,4,6...) custom-call(s32[1]{0:T(128)S(6)} %copy.15.spare, bf16[8,4,4,64,256]{4,3,2,1,0:T(8,128)(2,1)S(1)} %get-tuple-element.15.b13, ...), custom_call_target="tpu_custom_call" | custom-call | tf_op jit(solution)/shard_map/write/pallas_call | solution.py:396
Async XLA Ops:
  1.3 0.7 copy-start

commit v2 on v0

v2 whole, which is shorter than its diff:
```python
import jax
import jax.numpy as jnp
from jax import lax
from jax.experimental import pallas as pl
from jax.experimental.pallas import tpu as pltpu
from jax.sharding import PartitionSpec as P

MESH = pl.DeviceIdType.MESH
BF16 = jnp.bfloat16
RING = 4
UNIT_CHUNKS = 8
NEAR_CHUNKS = 8
NEAR_ROWS = 48
SIDE_ROWS = 16


def _exchange(gate, up, down, dense, hot, b, h, dn, u, give, take_in, cand, rza, ryb, sa, sb, rya, rzb, send, recv, local):
    x = lax.axis_index('stage')
    e = lax.axis_index('expert')
    z, y, c = e // 8, (e % 8) // 2, e % 2

    def ring(v):
        return lax.rem(v + RING, RING)

    def dev(xx, yy, zz, cc):
        return (ring(xx), ring(zz) * 8 + ring(yy) * 2 + cc)

    partner = dev(x, y, z, 1 - c)
    S_YZ, S_X, S_DENSE, S_HOT, S_MID, S_LOW = range(6)
    R_YZ = 0
    R_NEAR = R_YZ + RING * UNIT_CHUNKS
    R_FAR = R_NEAR + 2 * NEAR_CHUNKS
    R_AG2 = R_FAR + NEAR_CHUNKS
    R_AG3 = R_AG2 + 8
    R_X, R_CROSS, R_SIDE, R_DPASS, R_HPASS, R_SWAP, R_RS1, R_RS2, R_AGX, R_AG1 = range(R_AG3 + 4, R_AG3 + 14)

    def remote(src, dst, device, s, r):
        return pltpu.make_async_remote_copy(src_ref=src, dst_ref=dst, send_sem=send.at[s], recv_sem=recv.at[r],
                                            device_id=device, device_id_type=MESH)

    def same(ref, device, s, r):
        return remote(ref, ref, device, s, r)

    def settle(sem, like):
        pltpu.make_async_copy(like, like, sem).wait()

    stays = (z == y) & (c == y // 2)
    own_piece = 2 * (y % 2) + c

    def land(zs):
        return jnp.where(zs == x, x, RING + zs)

    loads = []
    for p in range(4):
        cols = pl.ds(p * 128, 128)
        loads.append(pltpu.make_async_copy(gate.at[:, :, :, cols], u.at[p, :, :, 0:64, 0:128], local.at[0]))
        loads.append(pltpu.make_async_copy(up.at[:, :, :, cols], u.at[p, :, :, 0:64, 128:256], local.at[0]))
        for a in range(4):
            loads.append(pltpu.make_async_copy(down.at[p, :, :, :, pl.ds(256 * a, 256)],
                                               u.at[p, :, :, pl.ds(64 + 8 * a, 8), :], local.at[0]))
    own_cols = pl.ds(pl.multiple_of(own_piece * 128, 128), 128)
    keep = [
        pltpu.make_async_copy(gate.at[:, :, :, own_cols], b.at[land(z), :, :, 0:64, 0:128], local.at[1]),
        pltpu.make_async_copy(up.at[:, :, :, own_cols], b.at[land(z), :, :, 0:64, 128:256], local.at[1]),
    ] + [
        pltpu.make_async_copy(down.at[own_piece, :, :, :, pl.ds(256 * a, 256)],
                              b.at[land(z), :, :, pl.ds(64 + 8 * a, 8), :], local.at[1]) for a in range(4)
    ]
    load_dense = pltpu.make_async_copy(dense, dn.at[x], local.at[2])
    for copy in loads:
        copy.start()
    load_dense.start()

    @pl.when(stays)
    def _():
        for copy in keep:
            copy.start()

    bar = pltpu.get_barrier_semaphore()

    def greet(device):
        pl.semaphore_signal(bar, inc=1, device_id=device, device_id_type=MESH)

    for zs in range(RING):
        @pl.when(jnp.logical_not(stays & (z == zs)))
        def _():
            greet(dev(x, z, zs, y // 2))
    for d in (1, 2, 3):
        greet(dev(x + d, y, z, c))
        greet(dev(x, y + d, z, c))
        greet(dev(x, y, z + d, c))
    greet(partner)

    settle(local.at[0], u)
    hot_c = hot[c]
    give[...] = u[hot[1 - c] % 4]
    pl.semaphore_wait(bar, jnp.where(stays, 13, 14))

    def part(ref, index, q):
        return ref.at[index, q // 2, pl.ds(2 * (q % 2), 2)]

    def yz_self(p):
        return stays & (own_piece == p)

    def yz_go(*chunks):
        for q in chunks:
            for p in range(4):
                @pl.when(jnp.logical_not(yz_self(p)))
                def _():
                    remote(part(u, p, q), part(b, land(z), q), dev(x, 2 * c + p // 2, y, p % 2),
                           S_YZ, R_YZ + z * UNIT_CHUNKS + q).start()

    def yz_arrive(zs, q):
        @pl.when(jnp.logical_not(stays & (zs == z)))
        def _():
            settle(recv.at[R_YZ + zs * UNIT_CHUNKS + q], part(b, land(zs), q))

        if q == 0:
            @pl.when(stays & (zs == z))
            def _():
                settle(local.at[1], b.at[0])

    def x_go(*chunks):
        for q in chunks:
            for d in (1, 3, 2):
                to = ring(x + d)
                yz_arrive(to, q)
                remote(part(b, RING + to, q), part(b, x, q), dev(x + d, y, z, c), S_X, R_X).start()

    def near(layer, j):
        return dn.at[ring(layer), c, pl.ds(NEAR_ROWS * j, NEAR_ROWS)]

    side_y = NEAR_ROWS * NEAR_CHUNKS + SIDE_ROWS * y
    side_z = NEAR_ROWS * NEAR_CHUNKS + SIDE_ROWS * (RING + z)

    def side(layer, start):
        return dn.at[ring(layer), c, pl.ds(pl.multiple_of(start, SIDE_ROWS), SIDE_ROWS)]

    half = NEAR_CHUNKS // 2

    def dense_wait():
        load_dense.wait()

    def dense_cross():
        for d in (1, 3, 2):
            for start in (side_y, side_z):
                same(side(x, start), dev(x + d, y, z, c), S_DENSE, R_CROSS).start()

    def dense_own(*chunks):
        for i in chunks:
            j = (i + half) % NEAR_CHUNKS
            same(near(x, i), dev(x + 1, y, z, c), S_DENSE, R_NEAR + i).start()
            same(near(x, j), dev(x - 1, y, z, c), S_DENSE, R_NEAR + NEAR_CHUNKS + j).start()

    def dense_side():
        settle(recv.at[R_CROSS], b.at[0, 0])
        for d in (1, 3, 2):
            for l in (1, 3, 2):
                same(side(x + l, side_y), dev(x, y + d, z, c), S_DENSE, R_SIDE).start()
                same(side(x + l, side_z), dev(x, y, z + d, c), S_DENSE, R_SIDE).start()

    def dense_side_end():
        settle(recv.at[R_SIDE], b.at[0, 0:3])
        for l in (1, 3, 2):
            same(dn.at[ring(x + l), c, pl.ds(NEAR_ROWS * NEAR_CHUNKS, 2 * RING * SIDE_ROWS)], partner, S_DENSE, R_DPASS).start()

    def dense_near(*chunks):
        for i in chunks:
            j = (i + half) % NEAR_CHUNKS
            settle(recv.at[R_NEAR + i], near(x - 1, i))
            if i < half:
                same(near(x - 1, i), dev(x + 1, y, z, c), S_DENSE, R_FAR + i).start()
            same(near(x - 1, i), partner, S_DENSE, R_DPASS).start()
            settle(recv.at[R_NEAR + NEAR_CHUNKS + j], near(x + 1, j))
            if j >= half:
                same(near(x + 1, j), dev(x - 1, y, z, c), S_DENSE, R_FAR + j).start()
            same(near(x + 1, j), partner, S_DENSE, R_DPASS).start()

    def dense_far():
        for j in range(NEAR_CHUNKS):
            settle(recv.at[R_FAR + j], near(x + 2, j))
            same(near(x + 2, j), partner, S_DENSE, R_DPASS).start()

    y_hot, z_hot = (hot_c // 8) % 4, hot_c // 32

    def hot_swap():
        remote(give, take_in, partner, S_HOT, R_SWAP).start()

    def hot_rs1():
        settle(recv.at[R_SWAP], take_in)
        cand[...] = jnp.where((hot_c // 4) % 2 == c, u[hot_c % 4], take_in[...])
        rza[z] = cand[:, z, 0:48]
        ryb[y] = cand[y, :, 48:96]
        for d in (1, 3, 2):
            remote(cand.at[:, ring(z + d), 0:48], rza.at[z], dev(x, y, z + d, c), S_MID, R_RS1).start()
            remote(cand.at[ring(y + d), :, 48:96], ryb.at[y], dev(x, y + d, z, c), S_MID, R_RS1).start()

    def hot_rs2():
        settle(recv.at[R_RS1], b.at[0, 0:3])
        sa[...] = rza[z_hot]
        sb[...] = ryb[y_hot]
        rya[y] = sa[y]
        rzb[z] = sb[z]
        for d in (1, 3, 2):
            remote(sa.at[ring(y + d)], rya.at[y], dev(x, y + d, z, c), S_LOW, R_RS2).start()
            remote(sb.at[ring(z + d)], rzb.at[z], dev(x, y, z + d, c), S_LOW, R_RS2).start()

    def hot_agx():
        settle(recv.at[R_RS2], b.at[0, 0, 0:3])
        h[c, x, y, z, 0:48] = rya[y_hot]
        h[c, x, y, z, 48:96] = rzb[z_hot]
        for d in (1, 3, 2):
            same(h.at[c, x, y, z], dev(x + d, y, z, c), S_LOW, R_AGX).start()

    def hot_ag1():
        settle(recv.at[R_AGX], b.at[0, 0, 0:3])
        for d in (1, 3, 2):
            same(h.at[c, 0:2, y, z], dev(x, y, z + d, c), S_MID, R_AG1).start()
            same(h.at[c, 2:4, y, z], dev(x, y + d, z, c), S_MID, R_AG1).start()

    def block(layer, d):
        if layer < 2:
            return h.at[c, layer, ring(y + d)]
        return h.at[c, layer, :, ring(z + d)]

    def along(layer, d):
        return dev(x, y + d, z, c) if layer < 2 else dev(x, y, z + d, c)

    def hot_ag2():
        settle(recv.at[R_AG1], b.at[0, 0:3])
        for lift in (0, 1):
            for l in (0, 2):
                same(block(l + lift, 0), along(l, 1), S_HOT, R_AG2 + l + lift).start()
                same(block(l + 1 - lift, 0), along(l, -1), S_HOT, R_AG2 + 4 + l + 1 - lift).start()
        for l in range(4):
            same(block(l, 0), partner, S_HOT, R_HPASS).start()

    def hot_ag3():
        for lift in (0, 1):
            for l in (0, 2):
                settle(recv.at[R_AG2 + l + lift], block(l + lift, -1))
                if lift == 0:
                    same(block(l, -1), along(l, 1), S_HOT, R_AG3 + l).start()
                same(block(l + lift, -1), partner, S_HOT, R_HPASS).start()
                settle(recv.at[R_AG2 + 4 + l + 1 - lift], block(l + 1 - lift, 1))
                if lift == 0:
                    same(block(l + 1, 1), along(l, -1), S_HOT, R_AG3 + l + 1).start()
                same(block(l + 1 - lift, 1), partner, S_HOT, R_HPASS).start()

    def hot_end():
        for l in range(4):
            settle(recv.at[R_AG3 + l], block(l, 2))
            same(block(l, 2), partner, S_HOT, R_HPASS).start()

    dense_wait()
    hot_swap()
    yz_go(0)
    dense_cross()
    dense_own(0, 1, 2, 3, 4, 5, 6, 7)
    hot_rs1()
    yz_go(1)
    hot_rs2()
    yz_go(2)
    hot_agx()
    yz_go(3)
    dense_near(0, 1, 2, 3, 4, 5, 6, 7)
    x_go(0, 1)
    hot_ag1()
    yz_go(4, 5)
    x_go(2)
    dense_side()
    x_go(3)
    hot_ag2()
    yz_go(6, 7)
    x_go(4, 5)
    dense_side_end()
    hot_ag3()
    x_go(6, 7)
    dense_far()
    hot_end()
    for q in range(UNIT_CHUNKS):
        yz_arrive(x, q)
    settle(recv.at[R_X], b.at[0:3])
    settle(recv.at[R_DPASS], b.at[0:4])
    settle(recv.at[R_HPASS], b.at[0:4])

    @pl.when(stays)
    def _():
        settle(send.at[S_YZ], b.at[0:3])

    @pl.when(jnp.logical_not(stays))
    def _():
        settle(send.at[S_YZ], b.at[0:4])

    settle(send.at[S_X], b.at[0:3])
    settle(send.at[S_DENSE], b)
    settle(send.at[S_HOT], b)
    settle(send.at[S_MID], b.at[0:2, 0:3])
    settle(send.at[S_LOW], b.at[0:2, 0, 0:3])


def _write(spare, b, h, dn, o13, o2, odn, osp13, osp2, zero13, zero2, sem):
    copies = [pltpu.make_async_copy(dn, odn, sem.at[0])]
    copies.append(pltpu.make_async_copy(b.at[0:4, :, :, 0:64], o13, sem.at[1]))
    for a in range(4):
        copies.append(pltpu.make_async_copy(b.at[0:4, :, :, pl.ds(64 + 8 * a, 8)], o2.at[:, :, :, :, pl.ds(256 * a, 256)], sem.at[2 + a]))
    for copy in copies:
        copy.start()
    slot = spare[0]

    @pl.when(slot >= 0)
    def _():
        fill = [pltpu.make_async_copy(h.at[slot, :, :, :, 0:64], osp13, sem.at[6])]
        for a in range(4):
            fill.append(pltpu.make_async_copy(h.at[slot, :, :, :, pl.ds(64 + 8 * a, 8)], osp2.at[:, :, :, :, pl.ds(256 * a, 256)], sem.at[7 + a]))
        for copy in fill:
            copy.start()
        for copy in fill:
            copy.wait()

    @pl.when(slot < 0)
    def _():
        zero13[...] = jnp.zeros_like(zero13)
        zero2[...] = jnp.zeros_like(zero2)
        fill = [pltpu.make_async_copy(zero13, osp13.at[l], sem.at[6 + l]) for l in range(4)]
        fill += [pltpu.make_async_copy(zero2, osp2.at[l], sem.at[10 + l]) for l in range(4)]
        for copy in fill:
            copy.start()
        for copy in fill:
            copy.wait()

    for copy in copies:
        copy.wait()


def solution(mesh):
    flat_axes = ('stage', 'expert')

    def local_move(w_gate, w_up, w_down, dense, hot_ids, spare_map):
        sources = (w_gate.reshape(4, 4, 64, 512), w_up.reshape(4, 4, 64, 512), w_down.reshape(4, 4, 4, 8, 1024),
                   dense.reshape(2, 512, 1024))
        hbm = pl.BlockSpec(memory_space=pltpu.HBM)
        vmem = pl.BlockSpec(memory_space=pltpu.VMEM)
        smem = pl.BlockSpec(memory_space=pltpu.SMEM)
        unit = (4, 4, 96, 256)
        moved = pl.pallas_call(
            _exchange,
            name='exchange',
            out_shape=(pltpu.VMEM((8,) + unit, BF16), pltpu.VMEM((2, 4) + unit, BF16), pltpu.VMEM((4, 2, 512, 1024), BF16)),
            in_specs=[hbm] * 4 + [smem],
            out_specs=[vmem] * 3,
            scratch_shapes=[
                pltpu.VMEM((4,) + unit, BF16), pltpu.VMEM(unit, BF16), pltpu.VMEM(unit, BF16), pltpu.VMEM(unit, BF16),
                pltpu.VMEM((4, 4, 48, 256), BF16), pltpu.VMEM((4, 4, 48, 256), BF16),
                pltpu.VMEM((4, 48, 256), BF16), pltpu.VMEM((4, 48, 256), BF16),
                pltpu.VMEM((4, 48, 256), BF16), pltpu.VMEM((4, 48, 256), BF16),
                pltpu.SemaphoreType.DMA((6,)),
                pltpu.SemaphoreType.DMA((4 * UNIT_CHUNKS + 3 * NEAR_CHUNKS + 22,)),
                pltpu.SemaphoreType.DMA((3,)),
            ],
            compiler_params=pltpu.CompilerParams(collective_id=0, has_side_effects=True, vmem_limit_bytes=16 * 2**20),
        )(*[pltpu.with_memory_space_constraint(part, pltpu.HBM) for part in sources], hot_ids)
        moved = [pltpu.with_memory_space_constraint(part, pltpu.VMEM) for part in moved]
        o13, o2, odn, osp13, osp2 = pl.pallas_call(
            _write,
            name='write',
            out_shape=(
                jax.ShapeDtypeStruct((4, 4, 4, 64, 256), BF16),
                jax.ShapeDtypeStruct((4, 4, 4, 8, 1024), BF16),
                jax.ShapeDtypeStruct((4, 2, 512, 1024), BF16),
                jax.ShapeDtypeStruct((4, 4, 4, 64, 256), BF16),
                jax.ShapeDtypeStruct((4, 4, 4, 8, 1024), BF16),
            ),
            in_specs=[smem] + [vmem] * 3,
            out_specs=[hbm] * 5,
            scratch_shapes=[pltpu.VMEM((4, 4, 64, 256), BF16), pltpu.VMEM((4, 4, 8, 1024), BF16), pltpu.SemaphoreType.DMA((14,))],
            compiler_params=pltpu.CompilerParams(vmem_limit_bytes=4 * 2**20),
        )(spare_map, *moved)
        return (o13.reshape(4, 1, 1024, 256), o2.reshape(4, 1, 128, 1024), odn.reshape(4, 1024, 1024),
                osp13.reshape(4, 1, 1024, 256), osp2.reshape(4, 1, 128, 1024))

    expert_spec = P('stage', 'expert', None, None)
    unit_spec = P(None, flat_axes, None, None)
    return jax.shard_map(
        local_move,
        mesh=mesh,
        in_specs=(expert_spec, expert_spec, expert_spec, P('stage', None, None), P(None), P(flat_axes)),
        out_specs=(unit_spec, unit_spec, P(None, None, None), unit_spec, unit_spec),
        check_vma=False,
    )
```

time: 460 us -> 89.8 us (0.20)
  the two profiles are of different devices: /device:TPU:127 before, /device:TPU:8 now
where the time goes in v2:
time: 89.8 us; the launch traced here: 88.5 us
  Pallas kernels  86.6 us (96%)
  between operations  1.3 us (1%)
    pallas_call x1, Pallas kernels, local_move(): pl.pallas_call(_exchange, name='exchange', out_shape=(pltpu.VMEM((8,) + u...  81.2 us
    pallas_call x1, Pallas kernels, local_move(): pl.pallas_call(_write, name='write', out_shape=(jax.ShapeDtypeStruct((4,...  5.41 us

profile of v2, /device:TPU:8, one launch (start us, length us, event | category | flops | bytes accessed | tf_op | source)
XLA Modules:
  0.0 88.5 jit_solution(2884189985318714214)
XLA Ops:
  1.3 0.0 copy-start
  1.3 0.6 copy-done
  1.9 81.2 %exchange.1 = (bf16[8,4,4,96,256]{4,3,2,1,0:T(8,128)(2,1)S(1)}, bf16[2,4,4,4,96,256]{5,4,3,2,1,0:T(8,128)(2,1)S(1)}, bf16[4,2,512,1024]{3,2,1,0:T(8,128)(2,1)S(1)}) custom-call(bf16[4,4,64,512]{3,2,1,0:T(8,128)(2,1)} %bitcast.18, bf16[4,4,64,512]{3,2,1,0:T(8,128)(2,1)} %bitcast.19, bf16[4,4,4,8,1024]{4,3,2,1,0:T(8,128)(2,1)} %bitcast.20, ...), custom_call_target="tpu_custom_call" | custom-call | tf_op jit(solution)/shard_map/exchange/pallas_call | solution.py:346
  83.1 5.4 %write.1 = (bf16[4,4,4,64,256]{4,3,2,1,0:T(8,128)(2,1)}, bf16[4,4,4,8,1024]{4,3,2,1,0:T(8,128)(2,1)}, bf16[4,2,512,1024]{3,2,1,0:T(8,128)(2,1)}, bf16[4,4,4,64,2...) custom-call(s32[1]{0:T(128)S(6)} %copy.15.spare, bf16[8,4,4,96,256]{4,3,2,1,0:T(8,128)(2,1)S(1)} %get-tuple-element.13.b, ...), custom_call_target="tpu_custom_call" | custom-call | tf_op jit(solution)/shard_map/write/pallas_call | solution.py:364
Async XLA Ops:
  1.3 0.7 copy-start

commit v3 on v2

--- a/solution.py
+++ b/solution.py
@@ -14,7 +14,7 @@
 SIDE_ROWS = 16
 
 
-def _exchange(gate, up, down, dense, hot, b, h, dn, u, give, take_in, cand, rza, ryb, sa, sb, rya, rzb, send, recv, local):
+def _exchange(gate, up, down, dense, hot_hbm, b, h, dn, u, give, take_in, cand, rza, ryb, sa, sb, rya, rzb, ids, send, recv, local):
     x = lax.axis_index('stage')
     e = lax.axis_index('expert')
     z, y, c = e // 8, (e % 8) // 2, e % 2
@@ -32,7 +32,8 @@
     R_FAR = R_NEAR + 2 * NEAR_CHUNKS
     R_AG2 = R_FAR + NEAR_CHUNKS
     R_AG3 = R_AG2 + 8
-    R_X, R_CROSS, R_SIDE, R_DPASS, R_HPASS, R_SWAP, R_RS1, R_RS2, R_AGX, R_AG1 = range(R_AG3 + 4, R_AG3 + 14)
+    R_SIDE = R_AG3 + 4
+    R_X, R_CROSS, R_TURN, R_DPASS, R_HPASS, R_SWAP, R_RS1, R_RS2, R_AGX, R_AG1 = range(R_SIDE + 4, R_SIDE + 14)
 
     def remote(src, dst, device, s, r):
         return pltpu.make_async_remote_copy(src_ref=src, dst_ref=dst, send_sem=send.at[s], recv_sem=recv.at[r],
@@ -67,6 +68,8 @@
                               b.at[land(z), :, :, pl.ds(64 + 8 * a, 8), :], local.at[1]) for a in range(4)
     ]
     load_dense = pltpu.make_async_copy(dense, dn.at[x], local.at[2])
+    load_ids = pltpu.make_async_copy(hot_hbm, ids, local.at[3])
+    load_ids.start()
     for copy in loads:
         copy.start()
     load_dense.start()
@@ -92,8 +95,9 @@
     greet(partner)
 
     settle(local.at[0], u)
-    hot_c = hot[c]
-    give[...] = u[hot[1 - c] % 4]
+    load_ids.wait()
+    hot_c = ids[c]
+    give[...] = u[ids[1 - c] % 4]
     pl.semaphore_wait(bar, jnp.where(stays, 13, 14))
 
     def part(ref, index, q):
@@ -130,11 +134,12 @@
     def near(layer, j):
         return dn.at[ring(layer), c, pl.ds(NEAR_ROWS * j, NEAR_ROWS)]
 
-    side_y = NEAR_ROWS * NEAR_CHUNKS + SIDE_ROWS * y
-    side_z = NEAR_ROWS * NEAR_CHUNKS + SIDE_ROWS * (RING + z)
-
-    def side(layer, start):
-        return dn.at[ring(layer), c, pl.ds(pl.multiple_of(start, SIDE_ROWS), SIDE_ROWS)]
+    def side(layer, axis, at, lanes=pl.ds(0, 1024)):
+        start = NEAR_ROWS * NEAR_CHUNKS + SIDE_ROWS * (RING * axis + ring(at))
+        return dn.at[ring(layer), c, pl.ds(pl.multiple_of(start, 8), SIDE_ROWS), lanes]
+
+    def beside(axis, d):
+        return dev(x, y, z + d, c) if axis else dev(x, y + d, z, c)
 
     half = NEAR_CHUNKS // 2
 
@@ -143,8 +148,8 @@
 
     def dense_cross():
         for d in (1, 3, 2):
-            for start in (side_y, side_z):
-                same(side(x, start), dev(x + d, y, z, c), S_DENSE, R_CROSS).start()
+            for axis, at in ((0, y), (1, z)):
+                same(side(x, axis, at), dev(x + d, y, z, c), S_DENSE, R_CROSS).start()
 
     def dense_own(*chunks):
         for i in chunks:
@@ -154,13 +159,21 @@
 
     def dense_side():
         settle(recv.at[R_CROSS], b.at[0, 0])
-        for d in (1, 3, 2):
-            for l in (1, 3, 2):
-                same(side(x + l, side_y), dev(x, y + d, z, c), S_DENSE, R_SIDE).start()
-                same(side(x + l, side_z), dev(x, y, z + d, c), S_DENSE, R_SIDE).start()
+        for axis, at in ((0, y), (1, z)):
+            for d in (1, -1):
+                for l in (1, 3, 2):
+                    same(side(x + l, axis, at), beside(axis, d), S_DENSE, R_SIDE + 2 * axis + (d + 1) // 2).start()
+
+    def dense_turn():
+        for axis, at in ((0, y), (1, z)):
+            for d in (1, -1):
+                settle(recv.at[R_SIDE + 2 * axis + (d + 1) // 2], b.at[0, 0, 0:2])
+                lanes = pl.ds(256 * (1 - d), 512)
+                for l in (1, 3, 2):
+                    same(side(x + l, axis, at - d, lanes), beside(axis, d), S_DENSE, R_TURN).start()
 
     def dense_side_end():
-        settle(recv.at[R_SIDE], b.at[0, 0:3])
+        settle(recv.at[R_TURN], b.at[0, 0])
         for l in (1, 3, 2):
             same(dn.at[ring(x + l), c, pl.ds(NEAR_ROWS * NEAR_CHUNKS, 2 * RING * SIDE_ROWS)], partner, S_DENSE, R_DPASS).start()
 
@@ -176,8 +189,8 @@
                 same(near(x + 1, j), dev(x - 1, y, z, c), S_DENSE, R_FAR + j).start()
             same(near(x + 1, j), partner, S_DENSE, R_DPASS).start()
 
-    def dense_far():
-        for j in range(NEAR_CHUNKS):
+    def dense_far(*chunks):
+        for j in chunks:
             settle(recv.at[R_FAR + j], near(x + 2, j))
             same(near(x + 2, j), partner, S_DENSE, R_DPASS).start()
 
@@ -235,8 +248,8 @@
         for l in range(4):
             same(block(l, 0), partner, S_HOT, R_HPASS).start()
 
-    def hot_ag3():
-        for lift in (0, 1):
+    def hot_ag3(*lifts):
+        for lift in lifts:
             for l in (0, 2):
                 settle(recv.at[R_AG2 + l + lift], block(l + lift, -1))
                 if lift == 0:
@@ -264,19 +277,19 @@
     hot_agx()
     yz_go(3)
     dense_near(0, 1, 2, 3, 4, 5, 6, 7)
+    dense_side()
     x_go(0, 1)
     hot_ag1()
     yz_go(4, 5)
-    x_go(2)
-    dense_side()
-    x_go(3)
-    hot_ag2()
+    x_go(2, 3)
+    dense_turn()
     yz_go(6, 7)
     x_go(4, 5)
+    hot_ag2()
+    x_go(6, 7)
+    hot_ag3(0, 1)
+    dense_far(0, 1, 2, 3, 4, 5, 6, 7)
     dense_side_end()
-    hot_ag3()
-    x_go(6, 7)
-    dense_far()
     hot_end()
     for q in range(UNIT_CHUNKS):
         yz_arrive(x, q)
@@ -347,19 +360,20 @@
             _exchange,
             name='exchange',
             out_shape=(pltpu.VMEM((8,) + unit, BF16), pltpu.VMEM((2, 4) + unit, BF16), pltpu.VMEM((4, 2, 512, 1024), BF16)),
-            in_specs=[hbm] * 4 + [smem],
+            in_specs=[hbm] * 5,
             out_specs=[vmem] * 3,
             scratch_shapes=[
                 pltpu.VMEM((4,) + unit, BF16), pltpu.VMEM(unit, BF16), pltpu.VMEM(unit, BF16), pltpu.VMEM(unit, BF16),
                 pltpu.VMEM((4, 4, 48, 256), BF16), pltpu.VMEM((4, 4, 48, 256), BF16),
                 pltpu.VMEM((4, 48, 256), BF16), pltpu.VMEM((4, 48, 256), BF16),
                 pltpu.VMEM((4, 48, 256), BF16), pltpu.VMEM((4, 48, 256), BF16),
+                pltpu.SMEM((2,), jnp.int32),
                 pltpu.SemaphoreType.DMA((6,)),
-                pltpu.SemaphoreType.DMA((4 * UNIT_CHUNKS + 3 * NEAR_CHUNKS + 22,)),
-                pltpu.SemaphoreType.DMA((3,)),
+                pltpu.SemaphoreType.DMA((4 * UNIT_CHUNKS + 3 * NEAR_CHUNKS + 26,)),
+                pltpu.SemaphoreType.DMA((4,)),
             ],
             compiler_params=pltpu.CompilerParams(collective_id=0, has_side_effects=True, vmem_limit_bytes=16 * 2**20),
-        )(*[pltpu.with_memory_space_constraint(part, pltpu.HBM) for part in sources], hot_ids)
+        )(*[pltpu.with_memory_space_constraint(part, pltpu.HBM) for part in (*sources, hot_ids)])
         moved = [pltpu.with_memory_space_constraint(part, pltpu.VMEM) for part in moved]
         o13, o2, odn, osp13, osp2 = pl.pallas_call(
             _write,

time: 89.8 us -> 83.7 us (0.932); the launches traced: 88.5 us -> 83.5 us
  Pallas kernels: 86.6 us -> 82.3 us
    pallas_call x1, Pallas kernels: 81.2 us -> 76.8 us  [local_move(): pl.pallas_call(_exchange, name='exchange', out_shape=(pltpu.VMEM((8,) + u...]
where the time goes in v3:
time: 83.7 us; the launch traced here: 83.5 us
  Pallas kernels  82.3 us (98%)
  between operations  1.29 us (2%)
    pallas_call x1, Pallas kernels, local_move(): pl.pallas_call(_exchange, name='exchange', out_shape=(pltpu.VMEM((8,) + u...  76.8 us
    pallas_call x1, Pallas kernels, local_move(): pl.pallas_call(_write, name='write', out_shape=(jax.ShapeDtypeStruct((4,...  5.41 us

profile of v3, /device:TPU:8, one launch (start us, length us, event | category | flops | bytes accessed | tf_op | source)
XLA Modules:
  0.0 83.5 jit_solution(9578955249920262904)
XLA Ops:
  1.3 76.8 %exchange.1 = (bf16[8,4,4,96,256]{4,3,2,1,0:T(8,128)(2,1)S(1)}, bf16[2,4,4,4,96,256]{5,4,3,2,1,0:T(8,128)(2,1)S(1)}, bf16[4,2,512,1024]{3,2,1,0:T(8,128)(2,1)S(1)}) custom-call(bf16[4,4,64,512]{3,2,1,0:T(8,128)(2,1)} %bitcast.18, bf16[4,4,64,512]{3,2,1,0:T(8,128)(2,1)} %bitcast.19, bf16[4,4,4,8,1024]{4,3,2,1,0:T(8,128)(2,1)} %bitcast.20, ...), custom_call_target="tpu_custom_call" | custom-call | tf_op jit(solution)/shard_map/exchange/pallas_call | solution.py:359
  78.1 5.4 %write.1 = (bf16[4,4,4,64,256]{4,3,2,1,0:T(8,128)(2,1)}, bf16[4,4,4,8,1024]{4,3,2,1,0:T(8,128)(2,1)}, bf16[4,2,512,1024]{3,2,1,0:T(8,128)(2,1)}, bf16[4,4,4,64,2...) custom-call(s32[1]{0:T(128)S(6)} %copy.15.spare, bf16[8,4,4,96,256]{4,3,2,1,0:T(8,128)(2,1)S(1)} %get-tuple-element.13.b, ...), custom_call_target="tpu_custom_call" | custom-call | tf_op jit(solution)/shard_map/write/pallas_call | solution.py:378

commit v4 on v3

--- a/solution.py
+++ b/solution.py
@@ -33,7 +33,8 @@
     R_AG2 = R_FAR + NEAR_CHUNKS
     R_AG3 = R_AG2 + 8
     R_SIDE = R_AG3 + 4
-    R_X, R_CROSS, R_TURN, R_DPASS, R_HPASS, R_SWAP, R_RS1, R_RS2, R_AGX, R_AG1 = range(R_SIDE + 4, R_SIDE + 14)
+    R_CROSS = R_SIDE + 4
+    R_X, R_OVER, R_TURN, R_DPASS, R_HPASS, R_SWAP, R_RS1, R_RS2, R_AGX, R_AG1 = range(R_CROSS + 2, R_CROSS + 12)
 
     def remote(src, dst, device, s, r):
         return pltpu.make_async_remote_copy(src_ref=src, dst_ref=dst, send_sem=send.at[s], recv_sem=recv.at[r],
@@ -147,9 +148,15 @@
         load_dense.wait()
 
     def dense_cross():
-        for d in (1, 3, 2):
+        for d in (1, -1):
             for axis, at in ((0, y), (1, z)):
-                same(side(x, axis, at), dev(x + d, y, z, c), S_DENSE, R_CROSS).start()
+                same(side(x, axis, at), dev(x + d, y, z, c), S_DENSE, R_CROSS + (d + 1) // 2).start()
+
+    def dense_over():
+        for d in (1, -1):
+            settle(recv.at[R_CROSS + (d + 1) // 2], dn.at[0, 0, 0:2 * SIDE_ROWS])
+            for axis, at in ((0, y), (1, z)):
+                same(side(x - d, axis, at, pl.ds(256 * (1 - d), 512)), dev(x + d, y, z, c), S_DENSE, R_OVER).start()
 
     def dense_own(*chunks):
         for i in chunks:
@@ -158,7 +165,7 @@
             same(near(x, j), dev(x - 1, y, z, c), S_DENSE, R_NEAR + NEAR_CHUNKS + j).start()
 
     def dense_side():
-        settle(recv.at[R_CROSS], b.at[0, 0])
+        settle(recv.at[R_OVER], dn.at[0, 0, 0:2 * SIDE_ROWS])
         for axis, at in ((0, y), (1, z)):
             for d in (1, -1):
                 for l in (1, 3, 2):
@@ -267,16 +274,18 @@
 
     dense_wait()
     hot_swap()
-    yz_go(0)
     dense_cross()
     dense_own(0, 1, 2, 3, 4, 5, 6, 7)
+    yz_go(0)
     hot_rs1()
     yz_go(1)
     hot_rs2()
+    dense_over()
     yz_go(2)
+    dense_near(0)
     hot_agx()
     yz_go(3)
-    dense_near(0, 1, 2, 3, 4, 5, 6, 7)
+    dense_near(1, 2, 3, 4, 5, 6, 7)
     dense_side()
     x_go(0, 1)
     hot_ag1()
@@ -286,10 +295,11 @@
     yz_go(6, 7)
     x_go(4, 5)
     hot_ag2()
-    x_go(6, 7)
+    x_go(6)
+    dense_far(0, 1, 2, 3, 4, 5, 6, 7)
+    x_go(7)
+    dense_side_end()
     hot_ag3(0, 1)
-    dense_far(0, 1, 2, 3, 4, 5, 6, 7)
-    dense_side_end()
     hot_end()
     for q in range(UNIT_CHUNKS):
         yz_arrive(x, q)
@@ -369,7 +379,7 @@
                 pltpu.VMEM((4, 48, 256), BF16), pltpu.VMEM((4, 48, 256), BF16),
                 pltpu.SMEM((2,), jnp.int32),
                 pltpu.SemaphoreType.DMA((6,)),
-                pltpu.SemaphoreType.DMA((4 * UNIT_CHUNKS + 3 * NEAR_CHUNKS + 26,)),
+                pltpu.SemaphoreType.DMA((4 * UNIT_CHUNKS + 3 * NEAR_CHUNKS + 28,)),
                 pltpu.SemaphoreType.DMA((4,)),
             ],
             compiler_params=pltpu.CompilerParams(collective_id=0, has_side_effects=True, vmem_limit_bytes=16 * 2**20),

time: 83.7 us -> 81.9 us (0.978); the launches traced: 83.5 us -> 80.9 us
  Pallas kernels: 82.3 us -> 79.6 us
    pallas_call x1, Pallas kernels: 76.8 us -> 74.2 us  [local_move(): pl.pallas_call(_exchange, name='exchange', out_shape=(pltpu.VMEM((8,) + u...]
where the time goes in v4:
time: 81.9 us; the launch traced here: 80.9 us
  Pallas kernels  79.6 us (97%)
  between operations  1.29 us (2%)
    pallas_call x1, Pallas kernels, local_move(): pl.pallas_call(_exchange, name='exchange', out_shape=(pltpu.VMEM((8,) + u...  74.2 us
    pallas_call x1, Pallas kernels, local_move(): pl.pallas_call(_write, name='write', out_shape=(jax.ShapeDtypeStruct((4,...  5.41 us

profile of v4, /device:TPU:8, one launch (start us, length us, event | category | flops | bytes accessed | tf_op | source)
XLA Modules:
  0.0 80.9 jit_solution(5120267727975603701)
XLA Ops:
  1.3 74.2 %exchange.1 = (bf16[8,4,4,96,256]{4,3,2,1,0:T(8,128)(2,1)S(1)}, bf16[2,4,4,4,96,256]{5,4,3,2,1,0:T(8,128)(2,1)S(1)}, bf16[4,2,512,1024]{3,2,1,0:T(8,128)(2,1)S(1)}) custom-call(bf16[4,4,64,512]{3,2,1,0:T(8,128)(2,1)} %bitcast.18, bf16[4,4,64,512]{3,2,1,0:T(8,128)(2,1)} %bitcast.19, bf16[4,4,4,8,1024]{4,3,2,1,0:T(8,128)(2,1)} %bitcast.20, ...), custom_call_target="tpu_custom_call" | custom-call | tf_op jit(solution)/shard_map/exchange/pallas_call | solution.py:369
  75.4 5.4 %write.1 = (bf16[4,4,4,64,256]{4,3,2,1,0:T(8,128)(2,1)}, bf16[4,4,4,8,1024]{4,3,2,1,0:T(8,128)(2,1)}, bf16[4,2,512,1024]{3,2,1,0:T(8,128)(2,1)}, bf16[4,4,4,64,2...) custom-call(s32[1]{0:T(128)S(6)} %copy.15.spare, bf16[8,4,4,96,256]{4,3,2,1,0:T(8,128)(2,1)S(1)} %get-tuple-element.13.b, ...), custom_call_target="tpu_custom_call" | custom-call | tf_op jit(solution)/shard_map/write/pallas_call | solution.py:388

commit v5 on v4

--- a/solution.py
+++ b/solution.py
@@ -34,7 +34,8 @@
     R_AG3 = R_AG2 + 8
     R_SIDE = R_AG3 + 4
     R_CROSS = R_SIDE + 4
-    R_X, R_OVER, R_TURN, R_DPASS, R_HPASS, R_SWAP, R_RS1, R_RS2, R_AGX, R_AG1 = range(R_CROSS + 2, R_CROSS + 12)
+    R_X, R_OVER, R_TURN, R_DPASS, R_HPASS, R_SWAP, R_RS1, R_RS2, R_AGX, R_AGF = range(R_CROSS + 2, R_CROSS + 12)
+    R_AG1 = R_CROSS + 12
 
     def remote(src, dst, device, s, r):
         return pltpu.make_async_remote_copy(src_ref=src, dst_ref=dst, send_sem=send.at[s], recv_sem=recv.at[r],
@@ -234,9 +235,17 @@
 
     def hot_ag1():
         settle(recv.at[R_AGX], b.at[0, 0, 0:3])
-        for d in (1, 3, 2):
-            same(h.at[c, 0:2, y, z], dev(x, y, z + d, c), S_MID, R_AG1).start()
-            same(h.at[c, 2:4, y, z], dev(x, y + d, z, c), S_MID, R_AG1).start()
+        for d in (1, -1):
+            same(h.at[c, 0:2, y, z], dev(x, y, z + d, c), S_MID, R_AG1 + (d + 1) // 2).start()
+            same(h.at[c, 2:4, y, z], dev(x, y + d, z, c), S_MID, R_AG1 + 2 + (d + 1) // 2).start()
+
+    def hot_again():
+        for d in (1, -1):
+            rows = pl.ds(24 * (1 - d), 48)
+            settle(recv.at[R_AG1 + (d + 1) // 2], b.at[0, 0, 0:2])
+            same(h.at[c, 0:2, y, ring(z - d), rows], dev(x, y, z + d, c), S_MID, R_AGF).start()
+            settle(recv.at[R_AG1 + 2 + (d + 1) // 2], b.at[0, 0, 0:2])
+            same(h.at[c, 2:4, ring(y - d), z, rows], dev(x, y + d, z, c), S_MID, R_AGF).start()
 
     def block(layer, d):
         if layer < 2:
@@ -247,7 +256,7 @@
         return dev(x, y + d, z, c) if layer < 2 else dev(x, y, z + d, c)
 
     def hot_ag2():
-        settle(recv.at[R_AG1], b.at[0, 0:3])
+        settle(recv.at[R_AGF], b.at[0, 0])
         for lift in (0, 1):
             for l in (0, 2):
                 same(block(l + lift, 0), along(l, 1), S_HOT, R_AG2 + l + lift).start()
@@ -274,9 +283,9 @@
 
     dense_wait()
     hot_swap()
+    yz_go(0)
     dense_cross()
     dense_own(0, 1, 2, 3, 4, 5, 6, 7)
-    yz_go(0)
     hot_rs1()
     yz_go(1)
     hot_rs2()
@@ -291,6 +300,7 @@
     hot_ag1()
     yz_go(4, 5)
     x_go(2, 3)
+    hot_again()
     dense_turn()
     yz_go(6, 7)
     x_go(4, 5)
@@ -379,7 +389,7 @@
                 pltpu.VMEM((4, 48, 256), BF16), pltpu.VMEM((4, 48, 256), BF16),
                 pltpu.SMEM((2,), jnp.int32),
                 pltpu.SemaphoreType.DMA((6,)),
-                pltpu.SemaphoreType.DMA((4 * UNIT_CHUNKS + 3 * NEAR_CHUNKS + 28,)),
+                pltpu.SemaphoreType.DMA((4 * UNIT_CHUNKS + 3 * NEAR_CHUNKS + 32,)),
                 pltpu.SemaphoreType.DMA((4,)),
             ],
             compiler_params=pltpu.CompilerParams(collective_id=0, has_side_effects=True, vmem_limit_bytes=16 * 2**20),

time: 81.9 us -> 81.6 us (level); the launches traced: 80.9 us -> 81.5 us
  no operation moved by 1% of the time
where the time goes in v5:
time: 81.6 us; the launch traced here: 81.5 us
  Pallas kernels  80.2 us (98%)
  between operations  1.29 us (2%)
    pallas_call x1, Pallas kernels, local_move(): pl.pallas_call(_exchange, name='exchange', out_shape=(pltpu.VMEM((8,) + u...  74.8 us
    pallas_call x1, Pallas kernels, local_move(): pl.pallas_call(_write, name='write', out_shape=(jax.ShapeDtypeStruct((4,...  5.41 us

profile of v5, /device:TPU:8, one launch (start us, length us, event | category | flops | bytes accessed | tf_op | source)
XLA Modules:
  0.0 81.5 jit_solution(2826960000509828276)
XLA Ops:
  1.3 74.8 %exchange.1 = (bf16[8,4,4,96,256]{4,3,2,1,0:T(8,128)(2,1)S(1)}, bf16[2,4,4,4,96,256]{5,4,3,2,1,0:T(8,128)(2,1)S(1)}, bf16[4,2,512,1024]{3,2,1,0:T(8,128)(2,1)S(1)}) custom-call(bf16[4,4,64,512]{3,2,1,0:T(8,128)(2,1)} %bitcast.18, bf16[4,4,64,512]{3,2,1,0:T(8,128)(2,1)} %bitcast.19, bf16[4,4,4,8,1024]{4,3,2,1,0:T(8,128)(2,1)} %bitcast.20, ...), custom_call_target="tpu_custom_call" | custom-call | tf_op jit(solution)/shard_map/exchange/pallas_call | solution.py:379
  76.1 5.4 %write.1 = (bf16[4,4,4,64,256]{4,3,2,1,0:T(8,128)(2,1)}, bf16[4,4,4,8,1024]{4,3,2,1,0:T(8,128)(2,1)}, bf16[4,2,512,1024]{3,2,1,0:T(8,128)(2,1)}, bf16[4,4,4,64,2...) custom-call(s32[1]{0:T(128)S(6)} %copy.15.spare, bf16[8,4,4,96,256]{4,3,2,1,0:T(8,128)(2,1)S(1)} %get-tuple-element.13.b, ...), custom_call_target="tpu_custom_call" | custom-call | tf_op jit(solution)/shard_map/write/pallas_call | solution.py:398
